TPU v7x, 512 devices: a 8x2x16 block of a 8x8x16 slice. The times are simulated.
512 devices in a mesh: subj: 2 (over y), row: 16 (over x, core), col: 16 (over z).
Axes of the slice: x: 8, y: 2, z: 16, core: 2. Of those that a mesh axis runs over, the one named last changes fastest.
The devices are a block of a 8x8x16 slice.
Arguments:
- series: float32 [800, 65536], P(None, ('subj', 'row', 'col')), parts along dimension 1, as said below
- keep_mask: int32 [512, 256], P(('subj', 'row'), 'col'), parts along dimension 0, may hold values from 0 to 1, as said below
- row_owner: int32 [512], P('subj'), parts along dimension 0, may hold values from 0 to 15, as said below
Outputs:
- owned_tiles: bfloat16 [32, 16, 96, 128, 128], P(('subj', 'row'), 'col'), parts along dimension 0
- owned_ids: int32 [32, 16, 96], P(('subj', 'row'), 'col'), parts along dimension 0
There are 2 independent parts, one for each index of `subj`. A program takes and returns all parts, laid end to end along the dimension named above; each array names one. Nothing has to cross between parts.
Inputs may be any that keep to these rules, and one draw needn't show every extreme that they name: Each voxel's series varies over time. `keep_mask`: of the 16 tiles that one tile row has in one column block, at most 6 are kept; in every draw one owner keeps exactly 6 in each of its tile rows in some column block. `row_owner`: the 16 tile rows of a row block have 16 different owners, and every owner holds 16 tile rows, from 16 different row blocks.
All inputs are finite; a program needn't handle non-finite values.
Results may differ from a plain program's by a relative error of at most 0.0042.
Values may be sent and summed in bfloat16 or wider, within the bound.
A program may use at most 64 MiB of HBM per device.

v0:
```python
import jax
import jax.numpy as jnp
from jax import lax
from jax.sharding import PartitionSpec as P

TILE = 128


epsilon = 1e-05


def compact(flat_tiles, flat_ids, capacity):
    is_valid = (flat_ids >= 0).astype(jnp.int32)
    running = jnp.cumsum(is_valid)
    slot_index = jnp.arange(capacity, dtype=jnp.int32)
    position = jnp.arange(flat_ids.shape[0], dtype=jnp.int32)
    slot_hit = (is_valid[None, :] == 1) & (running[None, :] == slot_index[:, None] + 1)
    picked = jnp.sum(jnp.where(slot_hit, position[None, :], 0), axis=1)
    present = running[-1] > slot_index
    chosen = jnp.take(flat_tiles, picked, axis=0)
    slot_tiles = jnp.where(present[:, None, None], chosen, jnp.zeros_like(chosen))
    slot_ids = jnp.where(present, jnp.take(flat_ids, picked), -1).astype(jnp.int32)
    return (slot_tiles, slot_ids)


def shards(series, keep_mask, row_owner):
    frames = series.shape[0]
    average = jnp.mean(series, axis=0, keepdims=True)
    centred = series - average
    spread = jnp.mean(centred * centred, axis=0, keepdims=True)
    scored = (centred * lax.rsqrt(spread + epsilon)).astype(jnp.bfloat16)
    row_block = lax.all_gather(scored, "col", axis=1, tiled=True)
    product = lax.dot_general(
        row_block,
        lax.all_gather(scored, "row", axis=1, tiled=True),
        (((0,), (0,)), ((), ())),
        preferred_element_type=jnp.float32,
    )
    tile_grid = (product * (1.0 / frames)).astype(jnp.bfloat16)
    row_count, col_count = keep_mask.shape
    tile_grid = tile_grid.reshape(row_count, TILE, col_count, TILE).transpose(0, 2, 1, 3)
    row_devices = lax.axis_size("row")
    col_devices = lax.axis_size("col")
    row_index = lax.axis_index("row")
    col_index = lax.axis_index("col")
    total_cols = col_count * col_devices
    slot_limit = max(2, 3 * col_count // 8)
    capacity = row_count * slot_limit
    local_owner = lax.dynamic_slice_in_dim(row_owner, row_index * row_count, row_count)
    targets = jnp.arange(row_devices, dtype=jnp.int32)
    owns_row = local_owner[None, :] == targets[:, None]
    has_row = jnp.any(owns_row, axis=1)
    row_of = jnp.sum(
        jnp.where(owns_row, jnp.arange(row_count, dtype=jnp.int32)[None, :], 0), axis=1
    )
    keep_flags = jnp.where(has_row[:, None], jnp.take(keep_mask, row_of, axis=0), 0)
    global_row = row_index * row_count + row_of
    first_col = col_index * col_count
    running = jnp.cumsum(keep_flags, axis=1)
    slot_index = jnp.arange(slot_limit, dtype=jnp.int32)
    slot_hit = (keep_flags[:, None, :] == 1) & (
        running[:, None, :] == slot_index[None, :, None] + 1
    )
    picked = jnp.sum(
        jnp.where(slot_hit, jnp.arange(col_count, dtype=jnp.int32)[None, None, :], 0), axis=2
    )
    present = running[:, -1:] > slot_index[None, :]
    chosen = tile_grid[row_of[:, None], picked]
    outgoing = jnp.where(present[:, :, None, None], chosen, jnp.zeros_like(chosen))
    out_ids = jnp.where(present, global_row[:, None] * total_cols + first_col + picked, -1)
    incoming, in_ids = (
        lax.all_to_all(outgoing, "row", split_axis=0, concat_axis=0, tiled=True),
        lax.all_to_all(out_ids, "row", split_axis=0, concat_axis=0, tiled=True),
    )
    flat_tiles = incoming.reshape(-1, TILE, TILE)
    flat_ids = in_ids.reshape(-1)
    slot_tiles, slot_ids = compact(flat_tiles, flat_ids, capacity)
    return (slot_tiles.reshape(1, 1, capacity, TILE, TILE), slot_ids.reshape(1, 1, capacity))


def solution(mesh):
    in_specs = (P(None, ("subj", "row", "col")), P(("subj", "row"), "col"), P("subj"))
    out_specs = (P(("subj", "row"), "col", None, None, None), P(("subj", "row"), "col", None))
    return jax.shard_map(shards, mesh=mesh, in_specs=in_specs, out_specs=out_specs, check_vma=False)
```

profile of v0, /device:TPU:65, one launch (start us, length us, event | category | flops | bytes accessed | tf_op | source)
XLA Modules:
  0.0 313.3 jit_solution(12894685114126903149)
XLA Ops:
  7.2 0.0 copy-start
  7.2 0.1 all-gather.3.cloned.1.call-start
  7.3 1.1 reduce_sum.60
  8.4 1.1 multiply_reduce_fusion
  9.5 1.7 multiply_convert_fusion.1
  11.3 0.1 all-gather.3.cloned.1.call-update
  11.3 0.1 all-gather.5.cloned.1.call-start
  11.4 0.7 all-gather.5.cloned.1.call-update
  12.1 0.8 dynamic_slice.3
  12.9 0.1 select_reduce_fusion.2
  13.0 0.0 copy-done
  13.0 0.6 gather_fusion
  13.6 0.1 fusion.3
  13.7 0.1 broadcast_compare_fusion
  13.8 0.2 reduce_window_sum.18
  14.0 0.2 slice_reduce_fusion
  14.2 0.3 select_reduce_fusion.1
  14.4 0.7 copy.18
  15.1 44.6 %all-to-all-start = ((s32[16,1,6]{2,1,0:T(1,128)}), s32[16,1,6]{2,1,0:T(1,128)S(1)}, u32[]{:S(2)}, u32[]{:S(2)}) async-start(s32[16,1,6]{2,1,0:T(1,128)} %copy.18), calls=%async_computation | async-start | bytes 16384 | tf_op jit(solution)/shard_map/all_to_all | solution.py:73
  59.8 0.1 copy.21
  59.9 0.1 reshape.311
  59.9 0.1 iota_compare_fusion
  60.0 64.0 %all-gather.3.cloned.1.call-done = bf16[800,2048]{1,0:T(8,128)(2,1)} async-done(((bf16[800,128]{1,0:T(8,128)(2,1)}), bf16[800,2048]{1,0:T(8,128)(2,1)}) %all-gather.3.cloned.1.call-update) | async-done | bytes 3276816 | tf_op jit(solution)/shard_map/all_gather | solution.py:32
  124.0 61.5 %all-gather.5.cloned.1.call-done = bf16[800,2048]{1,0:T(8,128)(2,1)} async-done(((bf16[800,128]{1,0:T(8,128)(2,1)}), bf16[800,2048]{1,0:T(8,128)(2,1)}) %all-gather.5.cloned.1.call-update) | async-done | bytes 3276816 | tf_op jit(solution)/shard_map/all_gather | solution.py:35
  185.5 13.6 %fusion = bf16[256,8,16,128]{3,1,2,0:T(8,128)(2,1)} fusion(bf16[800,2048]{1,0:T(8,128)(2,1)} %all-gather.3.cloned.1.call-done, bf16[800,2048]{1,0:T(8,128)(2,1)} %all-gather.5.cloned.1.call-done), kind=kOutput, calls=%fused_computation.6 | convolution fusion | flops 6719275008 | bytes 14942208 | tf_op jit(solution)/shard_map/dot_general | solution.py:33
  199.2 9.7 %copy.22 = bf16[256,8,16,128]{3,2,1,0:T(8,128)(2,1)} copy(bf16[256,8,16,128]{3,1,2,0:T(8,128)(2,1)} %fusion) | data formatting | bytes 16777216
  208.9 9.1 %copy.24 = bf16[16,128,16,128]{3,1,2,0:T(8,128)(2,1)} copy(bf16[16,128,16,128]{3,2,1,0:T(8,128)(2,1)} %bitcast.36) | data formatting | bytes 16777216 | tf_op jit(solution)/shard_map/reshape | solution.py:41
  218.0 4.9 %gather_fusion.1 = bf16[96,128,128]{2,1,0:T(8,128)(2,1)S(1)} fusion(bf16[16,16,128,128]{3,2,1,0:T(8,128)(2,1)} %bitcast.37, s32[96]{0:T(128)S(1)} %reshape.311), kind=kCustom, calls=%fused_computation.1 | custom fusion | bytes 6292224 | tf_op jit(solution)/shard_map/gather | solution.py:68
  223.0 1.9 broadcast_select_fusion
  224.9 0.0 all-to-all-done
  224.9 4.5 %all-to-all-start.1 = ((bf16[16,6,128,128]{3,2,1,0:T(8,128)(2,1)}), bf16[16,6,128,128]{3,2,1,0:T(8,128)(2,1)S(1)}, u32[]{:S(2)}, u32[]{:S(2)}) async-start(bf16[16,6,128,128]{3,2,1,0:T(8,128)(2,1)} %broadcast_select_fusion), calls=%async_computation.1 | async-start | bytes 6291456 | tf_op jit(solution)/shard_map/all_to_all | solution.py:72
  229.4 0.5 broadcast.364
  229.9 0.7 fusion.11
  230.6 0.1 reshape.333
  230.7 0.1 reduce-window.4
  230.8 0.1 reduce.3
  230.9 0.6 slice.21
  231.5 0.1 reshape.299
  231.6 0.2 select_reduce_fusion
  231.8 1.2 gather_fusion.3
  233.1 0.7 compare_and_fusion
  233.8 1.2 compare_select_fusion.6
  235.0 65.3 %all-to-all-done.1 = bf16[16,6,128,128]{3,2,1,0:T(8,128)(2,1)S(1)} async-done(((bf16[16,6,128,128]{3,2,1,0:T(8,128)(2,1)}), bf16[16,6,128,128]{3,2,1,0:T(8,128)(2,1)S(1)}, u32[]{:S(2)}, u32[]{:S(2)}) %all-to-all-start.1) | async-done | bytes 3145760 | tf_op jit(solution)/shard_map/all_to_all | solution.py:72
  300.3 2.7 gather_fusion.2
  303.0 3.4 %fusion.1 = bf16[1,1,96,128,128]{4,3,2,1,0:T(8,128)(2,1)} fusion(bf16[96,128,128]{2,1,0:T(8,128)(2,1)} %gather_fusion.2, pred[96]{0:T(512)(128)(4,1)S(1)} %get-tuple-element.8, pred[96]{0:T(512)(128)(4,1)S(1)} %get-tuple-element.9), kind=kLoop, calls=%fused_computation.8 | loop fusion | flops 3145728 | bytes 6291648 | tf_op jit(solution)/shard_map/jit(_where)/select_n | solution.py:21
  (13 shorter events, 0.1 us)
Async XLA Ops:
  7.2 5.9 %copy-start = (s32[16,16]{1,0:T(8,128)S(1)}, s32[16,16]{1,0:T(8,128)}, u32[]{:S(2)}) copy-start(s32[16,16]{1,0:T(8,128)} %param.4) | copy-start | bytes 3076
  7.2 116.8 %all-gather.3.cloned.1.call-start = ((), (), s32[]{:S(2)}) async-start(), calls=%async_computation.2 | async-start | bytes 3481600 | tf_op jit(solution)/shard_map/all_gather | solution.py:32
  11.3 174.2 %all-gather.5.cloned.1.call-start = ((), (), s32[]{:S(2)}) async-start(), calls=%async_computation.3 | async-start | bytes 3481600 | tf_op jit(solution)/shard_map/all_gather | solution.py:35
  15.1 209.8 %all-to-all-start = ((s32[16,1,6]{2,1,0:T(1,128)}), s32[16,1,6]{2,1,0:T(1,128)S(1)}, u32[]{:S(2)}, u32[]{:S(2)}) async-start(s32[16,1,6]{2,1,0:T(1,128)} %copy.18), calls=%async_computation | async-start | bytes 16384 | tf_op jit(solution)/shard_map/all_to_all | solution.py:73
  224.9 75.4 %all-to-all-start.1 = ((bf16[16,6,128,128]{3,2,1,0:T(8,128)(2,1)}), bf16[16,6,128,128]{3,2,1,0:T(8,128)(2,1)S(1)}, u32[]{:S(2)}, u32[]{:S(2)}) async-start(bf16[16,6,128,128]{3,2,1,0:T(8,128)(2,1)} %broadcast_select_fusion), calls=%async_computation.1 | async-start | bytes 6291456 | tf_op jit(solution)/shard_map/all_to_all | solution.py:72
Sparse Core Ops, SparseCore 0:
  11.4 112.5 all-gather.2
  126.6 58.8 all-gather.4
where the time goes:
time: 314 us; the launch traced here: 313 us
  waiting for transfers between devices  192 us (61%)
  starting transfers between devices  49.2 us (16%)
  local copies, waits for them, and re-layouts  31.4 us (10%)
  between operations  14.2 us (5%)
  matrix products  13.6 us (4%)
  other arithmetic  13.2 us (4%)
    all_to_all x1, waiting for transfers between devices, shards(): lax.all_to_all(outgoing, 'row', split_axis=0, concat_axis=0, tiled=True)  65.3 us
    all_gather x1, waiting for transfers between devices, shards(): row_block = lax.all_gather(scored, 'col', axis=1, tiled=True)  64 us
    all_gather x1, waiting for transfers between devices, shards(): lax.all_gather(scored, 'row', axis=1, tiled=True)  61.5 us
    all_to_all x1, starting transfers between devices, shards(): lax.all_to_all(out_ids, 'row', split_axis=0, concat_axis=0, tiled=True)  44.6 us
    dot_general x1, matrix products, shards(): lax.dot_general(row_block, lax.all_gather(scored, 'row', axis=1, tiled=Tr...  13.6 us
    unnamed x3, local copies, waits for them, and re-layouts  9.76 us
    reshape x1, local copies, waits for them, and re-layouts, shards(): tile_grid.reshape(row_count, TILE, col_count, TILE).transpose(0, 2, 1, 3)  9.11 us
  transfers between devices with their start and end apart: 4, of which 3 were waited for; matrix products, arithmetic and copies ran while one was open for 15% of the time, Pallas kernels for 0%

commit v1 on v0

v1 whole, which is shorter than its diff:
```python
import functools

import jax
import jax.numpy as jnp
from jax import lax
from jax.experimental import pallas as pl
from jax.experimental.pallas import tpu as pltpu
from jax.sharding import PartitionSpec as P

MESH = pl.DeviceIdType.MESH
EPSILON = 1e-05
UNIT = 16
GROUPS = 2
PIECES = 4


def cut(first, size, parts):
    units = size // UNIT
    edges = [first + UNIT * (units * p // parts) for p in range(parts)] + [first + size]
    return [(a, b - a) for a, b in zip(edges[:-1], edges[1:])]


def move(
    rows,
    cols,
    groups,
    series_ref,
    keep_ref,
    owner_ref,
    left_ref,
    right_ref,
    flags_ref,
    *scratch,
):
    gathered, outbox = scratch[: len(groups)], scratch[len(groups) : 2 * len(groups)]
    keeps = scratch[2 * len(groups)]
    z_send, z_recv, x_send, x_recv, d_send, d_recv, a_send, a_recv, e_send, e_recv, k_send, k_recv = scratch[
        2 * len(groups) + 1 :
    ]
    chips = rows // 2
    row, col = lax.axis_index("row"), lax.axis_index("col")
    core, chip = lax.rem(row, 2), lax.div(row, 2)
    up, down = lax.rem(col + 1, cols), lax.rem(col + cols - 1, cols)
    partner = row + 1 - 2 * core

    def chip_at(offset):
        return lax.rem(chip + offset + chips, chips)

    def col_at(offset):
        return lax.rem(col + offset + cols, cols)

    def copy(src, dst, send, recv, to_row, to_col):
        return pltpu.make_async_remote_copy(
            src_ref=src,
            dst_ref=dst,
            send_sem=send,
            recv_sem=recv,
            device_id={"row": to_row, "col": to_col},
            device_id_type=MESH,
        )

    barrier = pltpu.get_barrier_semaphore()
    for offset in range(1, rows):
        pl.semaphore_signal(
            barrier, inc=1, device_id={"row": lax.rem(row + offset, rows), "col": col}, device_id_type=MESH
        )
    for to_col in (up, down):
        pl.semaphore_signal(barrier, inc=1, device_id={"row": row, "col": to_col}, device_id_type=MESH)

    frames = series_ref.shape[0]
    series = series_ref[...]
    centred = series - jnp.sum(series, axis=0, keepdims=True) * (1.0 / frames)
    spread = jnp.sum(centred * centred, axis=0, keepdims=True) * (1.0 / frames)
    scored = (centred * lax.rsqrt(spread + EPSILON)).astype(jnp.bfloat16)
    for g, pieces in enumerate(groups):
        first, size = pieces[0][0], sum(s for _, s in pieces)
        gathered[g][col] = scored[first : first + size]
    right_ref[row] = scored
    keeps[row] = keep_ref[...]

    pl.semaphore_wait(barrier, rows + 1)

    z_pieces = [(g, i, *piece) for g, pieces in enumerate(groups) for i, piece in enumerate(pieces)]
    x_pieces = [(pieces[0][0], sum(s for _, s in pieces)) for pieces in groups]

    def z_hops(n, way):
        return cols // 2 if n % 2 == way else cols - 1 - cols // 2

    def x_hops(n, way):
        return chips // 2 if n % 2 == way else chips - 1 - chips // 2

    def z_copy(n, way, hop):
        g, _, first, size = z_pieces[n]
        origin = col_at(1 - hop if way == 0 else hop - 1)
        part = gathered[g].at[origin, pl.ds(first - groups[g][0][0], size)]
        return copy(part, part, z_send.at[n, way, hop - 1], z_recv.at[n, way, hop - 1], row, up if way == 0 else down)

    def x_copy(n, way, hop):
        first, size = x_pieces[n]
        origin = 2 * chip_at(1 - hop if way == 0 else hop - 1) + core
        part = right_ref.at[origin, pl.ds(first, size)]
        to_row = 2 * chip_at(1 if way == 0 else -1) + core
        return copy(part, part, x_send.at[n, way, hop - 1], x_recv.at[n, way, hop - 1], to_row, col)

    def d_copy(n, offset):
        first, size = x_pieces[n]
        part = right_ref.at[2 * chip_at(offset) + core, pl.ds(first, size)]
        return copy(part, part, d_send.at[n, offset], d_recv.at[n, offset], partner, col)

    def k_copy(offset):
        return copy(
            keep_ref, keeps.at[row], k_send.at[offset], k_recv.at[offset], lax.rem(row + offset, rows), col
        )

    def z_start(g):
        for n, piece in enumerate(z_pieces):
            if piece[0] == g:
                for way in range(2):
                    z_copy(n, way, 1).start()

    def z_step(g, hop):
        for n, piece in enumerate(z_pieces):
            if piece[0] == g:
                for way in range(2):
                    if hop <= z_hops(n, way):
                        z_copy(n, way, hop).wait_recv()
                        if hop < z_hops(n, way):
                            z_copy(n, way, hop + 1).start()

    def x_step(hop):
        for n in range(len(x_pieces)):
            for way in range(2):
                if hop <= x_hops(n, way):
                    x_copy(n, way, hop).wait_recv()
                    if hop < x_hops(n, way):
                        x_copy(n, way, hop + 1).start()
                    d_copy(n, chips - hop if way == 0 else hop).start()

    same = lax.rem(col, 2) == 0
    to_core = lax.rem(row + col, 2)
    offsets = [0] + sorted(range(1, chips), key=lambda o: (min(o, chips - o), o))
    to_up = offsets[::2]

    def a_copy(g, offset):
        first, size = groups[g][0][0], sum(s for _, s in groups[g])
        return copy(
            outbox[g].at[offset],
            left_ref.at[row, pl.ds(first, size)],
            a_send.at[g, offset],
            a_recv.at[g, offset],
            2 * chip_at(offset) + to_core,
            col,
        )

    def picked(offset):
        owner = 2 * chip_at(offset) + to_core
        place = jnp.int32(0)
        for i in range(cols):
            place = jnp.where(owner_ref[row * cols + i] == owner, i, place)
        return place

    def a_start(g):
        first, size = groups[g][0][0], sum(s for _, s in groups[g])
        for offset in offsets[1:] + [0]:
            place = picked(offset)
            if offset:
                outbox[g][offset] = gathered[g][place]
                a_copy(g, offset).start()
            else:

                @pl.when(same)
                def _():
                    left_ref[row, pl.ds(first, size)] = gathered[g][place]

                @pl.when(jnp.logical_not(same))
                def _():
                    outbox[g][offset] = gathered[g][place]
                    a_copy(g, offset).start()

    def e_copy(g, offset):
        first, size = groups[g][0][0], sum(s for _, s in groups[g])
        part = left_ref.at[2 * chip_at(-offset) + to_core, pl.ds(first, size)]
        return copy(part, part, e_send.at[g, offset], e_recv.at[g, offset], row, up if offset in to_up else down)

    def e_start(g):
        for offset in offsets:
            if offset:
                a_copy(g, offset).wait_recv()
            else:

                @pl.when(jnp.logical_not(same))
                def _():
                    a_copy(g, offset).wait_recv()

            e_copy(g, offset).start()

    last = cols // 2
    z_start(0)
    for n in range(len(x_pieces)):
        for way in range(2):
            x_copy(n, way, 1).start()
    for offset in range(1, rows):
        k_copy(offset).start()
    for n in range(len(x_pieces)):
        d_copy(n, 0).start()
    for g in range(len(groups)):
        for hop in range(1, last):
            z_step(g, hop)
            if g == 0 and hop % 2 == 0:
                x_step(hop // 2)
        if g + 1 < len(groups):
            z_start(g + 1)
        z_step(g, last)
        if g == 0:
            for hop in range(last // 2, chips // 2 + 1):
                x_step(hop)
        a_start(g)
        if g:
            e_start(g - 1)
    e_start(len(groups) - 1)

    for offset in range(1, rows):
        k_copy(offset).wait_recv()
    for k in range(rows):
        place = jnp.int32(0)
        for i in range(cols):
            place = jnp.where(owner_ref[k * cols + i] == row, i, place)
        flags_ref[pl.ds(k, 1), :] = keeps[k, pl.ds(place, 1), :]
    for n in range(len(x_pieces)):
        for offset in range(chips):
            d_copy(n, offset).wait_recv()
    for g in range(len(groups)):
        for offset in range(chips):
            e_copy(g, offset).wait_recv()

    for n in range(len(z_pieces)):
        for way in range(2):
            for hop in range(1, z_hops(n, way) + 1):
                z_copy(n, way, hop).wait_send()
    for n in range(len(x_pieces)):
        for way in range(2):
            for hop in range(1, x_hops(n, way) + 1):
                x_copy(n, way, hop).wait_send()
        for offset in range(chips):
            d_copy(n, offset).wait_send()
    for offset in range(1, rows):
        k_copy(offset).wait_send()
    for g in range(len(groups)):
        for offset in range(chips):
            if offset:
                a_copy(g, offset).wait_send()
            else:

                @pl.when(jnp.logical_not(same))
                def _():
                    a_copy(g, offset).wait_send()

            e_copy(g, offset).wait_send()


def multiply(capacity, limit, left_ref, right_ref, flags_ref, owner_ref, tiles_ref, ids_ref, packed, ids, places, sem):
    rows, frames, tile = left_ref.shape
    cols = flags_ref.shape[1]
    row, col = lax.axis_index("row"), lax.axis_index("col")
    total_cols = cols * lax.axis_size("col")
    first_col = col * cols
    for i in range(cols + 1):
        places[i] = 0

    def one_row(k, start):
        count = jnp.int32(0)
        for j in range(cols):
            places[count] = j
            count += flags_ref[k, j]
        place = jnp.int32(0)
        for i in range(cols):
            place = jnp.where(owner_ref[k * cols + i] == row, i, place)
        base = (k * cols + place) * total_cols + first_col
        rows_of = left_ref[k]
        for s in range(0, limit, 2):
            a, b = places[s], places[s + 1]
            product = lax.dot_general(
                rows_of,
                jnp.concatenate([right_ref[a], right_ref[b]], axis=1),
                (((0,), (0,)), ((), ())),
                preferred_element_type=jnp.float32,
            ) * (1.0 / frames)
            packed[start + s] = product[:, :tile].astype(packed.dtype)
            packed[start + s + 1] = product[:, tile:].astype(packed.dtype)
            ids[start + s] = base + a
            ids[start + s + 1] = base + b
        return start + count

    total = lax.fori_loop(0, rows, one_row, jnp.int32(0))

    def blank(s, carry):
        packed[s] = jnp.zeros_like(packed[s])
        ids[s] = -1
        return carry

    lax.fori_loop(total, capacity, blank, 0)
    out = pltpu.make_async_copy(packed.at[pl.ds(0, capacity)], tiles_ref, sem)
    out.start()
    for s in range(capacity):
        ids_ref[s] = ids[s]
    out.wait()


def shards(series, keep_mask, row_owner):
    frames, tile = series.shape
    row_count, col_count = keep_mask.shape
    rows, cols = lax.axis_size("row"), lax.axis_size("col")
    limit = max(2, 3 * col_count // 8)
    capacity = row_count * limit
    groups = [cut(first, size, PIECES) for first, size in cut(0, frames, GROUPS)]
    sizes = [sum(s for _, s in pieces) for pieces in groups]
    n_z, n_g = sum(len(pieces) for pieces in groups), len(groups)
    chips = rows // 2
    vmem, smem = pl.BlockSpec(memory_space=pltpu.VMEM), pl.BlockSpec(memory_space=pltpu.SMEM)
    dma = pltpu.SemaphoreType.DMA
    left, right, flags = pl.pallas_call(
        functools.partial(move, rows, cols, groups),
        out_shape=(
            jax.ShapeDtypeStruct((rows, frames, tile), jnp.bfloat16),
            jax.ShapeDtypeStruct((rows, frames, tile), jnp.bfloat16),
            jax.ShapeDtypeStruct((rows, col_count), jnp.int32),
        ),
        in_specs=[vmem, vmem, smem],
        out_specs=(vmem, vmem, vmem),
        scratch_shapes=[
            *[pltpu.VMEM((cols, size, tile), jnp.bfloat16) for size in sizes],
            *[pltpu.VMEM((chips, size, tile), jnp.bfloat16) for size in sizes],
            pltpu.VMEM((rows, row_count, col_count), jnp.int32),
            *[dma((n_z, 2, cols // 2))] * 2,
            *[dma((n_g, 2, chips // 2))] * 2,
            *[dma((n_g, chips))] * 2,
            *[dma((n_g, chips))] * 2,
            *[dma((n_g, chips))] * 2,
            *[dma((rows,))] * 2,
        ],
        compiler_params=pltpu.CompilerParams(collective_id=0, has_side_effects=True, vmem_limit_bytes=24 * 2**20),
    )(series, keep_mask, row_owner)
    tiles, ids = pl.pallas_call(
        functools.partial(multiply, capacity, limit),
        out_shape=(
            jax.ShapeDtypeStruct((capacity, tile, tile), jnp.bfloat16),
            jax.ShapeDtypeStruct((capacity,), jnp.int32),
        ),
        in_specs=[vmem, vmem, smem, smem],
        out_specs=(pl.BlockSpec(memory_space=pl.ANY), smem),
        scratch_shapes=[
            pltpu.VMEM((capacity + limit, tile, tile), jnp.bfloat16),
            pltpu.SMEM((capacity + limit,), jnp.int32),
            pltpu.SMEM((col_count + 1,), jnp.int32),
            dma(()),
        ],
        compiler_params=pltpu.CompilerParams(vmem_limit_bytes=24 * 2**20),
    )(left, right, flags, row_owner)
    return tiles.reshape(1, 1, capacity, tile, tile), ids.reshape(1, 1, capacity)


def solution(mesh):
    in_specs = (P(None, ("subj", "row", "col")), P(("subj", "row"), "col"), P("subj"))
    out_specs = (P(("subj", "row"), "col", None, None, None), P(("subj", "row"), "col", None))
    return jax.shard_map(shards, mesh=mesh, in_specs=in_specs, out_specs=out_specs, check_vma=False)
```

time: 314 us -> 136 us (0.43)
  waiting for transfers between devices: 192 us -> 0 us
  Pallas kernels: 0 us -> 132 us
  starting transfers between devices: 49.2 us -> 0 us
  local copies, waits for them, and re-layouts: 31.4 us -> 2.37 us
  matrix products: 13.6 us -> 0 us
  between operations: 14.2 us -> 0.65 us
  other arithmetic: 13.2 us -> 0 us
    pallas_call x0 -> x2, Pallas kernels: none -> 132 us  [the longest x1 122 us: shards(): pl.pallas_call(functools.partial(move, rows, cols, groups), out_shape=(ja...]
    all_gather x2 -> x0, waiting for transfers between devices: 125 us -> none  [the longest x1 64 us: shards(): row_block = lax.all_gather(scored, 'col', axis=1, tiled=True)]
    all_to_all x2 -> x0, waiting for transfers between devices: 65.3 us -> none  [the longest x1 65.3 us: shards(): lax.all_to_all(outgoing, 'row', split_axis=0, concat_axis=0, tiled=True)]
    all_to_all x2 -> x0, starting transfers between devices: 49.1 us -> none  [the longest x1 44.6 us: shards(): lax.all_to_all(out_ids, 'row', split_axis=0, concat_axis=0, tiled=True)]
    dot_general x1 -> x0, matrix products: 13.6 us -> none  [shards(): lax.dot_general(row_block, lax.all_gather(scored, 'row', axis=1, tiled=Tr...]
    gather x4 -> x0, local copies, waits for them, and re-layouts: 9.43 us -> none  [the longest x1 4.92 us: shards(): chosen = tile_grid[row_of[:, None], picked]]
    reshape x2 -> x0, local copies, waits for them, and re-layouts: 9.19 us -> none  [the longest x1 9.11 us: shards(): tile_grid.reshape(row_count, TILE, col_count, TILE).transpose(0, 2, 1, 3)]
    unnamed x3 -> x6, local copies, waits for them, and re-layouts: 9.76 us -> 2.37 us
  transfers between devices with their start and end apart: 4 -> 0, of which waited for: 3 -> 0; matrix products, arithmetic and copies ran while one was open for 15% -> 0% of each run, Pallas kernels for 0% -> 0%
where the time goes in v1:
time: 136 us; the launch traced here: 135 us
  Pallas kernels  132 us (97%)
  local copies, waits for them, and re-layouts  2.37 us (2%)
    pallas_call x1, Pallas kernels, shards(): pl.pallas_call(functools.partial(move, rows, cols, groups), out_shape=(ja...  122 us
    pallas_call x1, Pallas kernels, shards(): pl.pallas_call(functools.partial(multiply, capacity, limit), out_shape=(j...  9.81 us

profile of v1, /device:TPU:65, one launch (start us, length us, event | category | flops | bytes accessed | tf_op | source)
XLA Modules:
  0.0 134.5 jit_solution(1918709522385476980)
XLA Ops:
  0.6 0.0 copy-start
  0.6 1.0 copy-done
  1.6 0.0 copy-start.1
  1.6 0.7 copy-done.1
  2.3 0.0 copy-start.2
  2.3 0.7 copy-done.2
  3.0 121.7 %shard_map.50 = (bf16[16,800,128]{2,1,0:T(8,128)(2,1)S(1)}, bf16[16,800,128]{2,1,0:T(8,128)(2,1)S(1)}, s32[16,16]{1,0:T(8,128)S(1)}) custom-call(f32[800,128]{1,0:T(8,128)S(1)} %copy-done, s32[16,16]{1,0:T(8,128)S(1)} %copy-done.1, s32[256]{0:T(256)S(1)} %copy-done.2), custom_call_target="tpu_custom_call" | custom-call | tf_op jit(solution)/shard_map/pallas_call | solution.py:321
  124.7 9.8 %shard_map.51 = (bf16[96,128,128]{2,1,0:T(8,128)(2,1)}, s32[96]{0:T(128)}) custom-call(bf16[16,800,128]{2,1,0:T(8,128)(2,1)S(1)} %get-tuple-element.7.left_ref, bf16[16,800,128]{2,1,0:T(8,128)(2,1)S(1)} %get-tuple-element.8.right_ref, s32[16,16]{1,0:T(8,128)S(1)} %get-tuple-element.9.flags_ref, s32[256]{0:T(256)S(1)} %copy-done.2), custom_call_target="tpu_custom_call" | custom-call | tf_op jit(solution)/shard_map/pallas_call | solution.py:343
Async XLA Ops:
  0.6 1.0 copy-start
  1.6 0.7 copy-start.1
  2.3 0.7 copy-start.2

commit v2 on v1

v2 whole, which is shorter than its diff:
```python
import functools

import jax
import jax.numpy as jnp
from jax import lax
from jax.experimental import pallas as pl
from jax.experimental.pallas import tpu as pltpu
from jax.sharding import PartitionSpec as P

MESH = pl.DeviceIdType.MESH
EPSILON = 1e-05
UNIT = 16
GROUPS = 4
X_PIECES = 2
BEHIND = 6
STEP, HOP, BLOCK = 2.6, 2.6, 4.4


def cut(first, size, parts):
    units = size // UNIT
    edges = [first + UNIT * (units * p // parts) for p in range(parts)] + [first + size]
    return [(a, b - a) for a, b in zip(edges[:-1], edges[1:])]


def arrivals(cols, chips, behind, ahead):
    last = cols - 1
    start = [STEP * c + 4.0 for c in range(cols)]
    up = [[1e9] * (behind + 1) for _ in range(cols)]
    down = [[1e9] * (ahead + 1) for _ in range(cols)]
    for _ in range(4 * cols):
        for c in range(cols):
            above, below = (c + 1) % cols, (c - 1) % cols
            for i in range(1, ahead + 1):
                ready = start[above] if i == 1 else down[above][i - 1]
                if above == 0:
                    ready = max(ready, up[0][1])
                queue = down[c][i - 1] - HOP + BLOCK if i > 1 else 0.0
                down[c][i] = max(ready, queue) + HOP
            for h in range(1, behind + 1):
                if c == 0:
                    ready = start[cols - h]
                else:
                    ready = max(start[below] if h == 1 else up[below][h - 1], down[below][1] if below != last else 0.0)
                queue = up[c][h - 1] - HOP + BLOCK if h > 1 and c else 0.0
                up[c][h] = max(ready, queue) + HOP
    turns = []
    for c in range(cols):
        floor = 0 if c == last else 1
        from_behind = [max(floor, sum(down[c][i] <= up[c][h] for i in range(1, ahead + 1))) for h in range(1, behind + 1)]
        along = [sum(down[c][i] <= start[c] + BLOCK * h for i in range(1, ahead + 1)) for h in range(1, chips // 2 + 1)]
        for turn in (from_behind, along):
            for h in range(1, len(turn)):
                turn[h] = max(turn[h], turn[h - 1])
        turns.append((from_behind, along))
    return turns


def move(
    rows,
    cols,
    groups,
    series_hbm,
    keep_hbm,
    owner_hbm,
    left_ref,
    right_ref,
    flags_ref,
    spots_ref,
    *scratch,
):
    n_g = len(groups)
    gathered, outbox = scratch[:n_g], scratch[n_g : 2 * n_g]
    series_ref, keep_ref, owner_ref, keeps, load = scratch[2 * n_g : 2 * n_g + 5]
    (
        up_send,
        up_recv,
        down_send,
        down_recv,
        far_send,
        x_send,
        x_recv,
        d_send,
        d_recv,
        a_send,
        a_recv,
        e_send,
        e_recv,
        f_send,
        k_send,
        k_recv,
    ) = scratch[2 * n_g + 5 :]
    chips = rows // 2
    row, col = lax.axis_index("row"), lax.axis_index("col")
    core, chip = lax.rem(row, 2), lax.div(row, 2)
    last = cols - 1
    behind = BEHIND
    ahead = cols - 1 - behind
    above, below = lax.rem(col + 1, cols), lax.rem(col + cols - 1, cols)
    partner = row + 1 - 2 * core
    is_first, is_last = col == 0, col == last

    def when(condition, do):
        pl.when(condition)(do)

    def chip_at(offset):
        return lax.rem(chip + offset + chips, chips)

    def col_at(offset):
        return lax.rem(col + offset + cols, cols)

    def greet(to_row, to_col):
        pl.semaphore_signal(
            pltpu.get_barrier_semaphore(), inc=1, device_id={"row": to_row, "col": to_col}, device_id_type=MESH
        )

    def copy(src, dst, send, recv, to_row, to_col):
        return pltpu.make_async_remote_copy(
            src_ref=src,
            dst_ref=dst,
            send_sem=send,
            recv_sem=recv,
            device_id={"row": to_row, "col": to_col},
            device_id_type=MESH,
        )

    loads = [
        pltpu.make_async_copy(src, dst, load.at[i])
        for i, (src, dst) in enumerate(((series_hbm, series_ref), (owner_hbm, owner_ref), (keep_hbm, keep_ref)))
    ]
    for one in loads:
        one.start()

    barrier = pltpu.get_barrier_semaphore()
    greet(2 * chip_at(1) + core, col)
    greet(2 * chip_at(-1) + core, col)
    greet(partner, col)
    pl.when(is_first)(lambda: greet(row, last))

    loads[0].wait()
    frames = series_ref.shape[0]
    series = series_ref[...]
    centred = series - jnp.sum(series, axis=0, keepdims=True) * (1.0 / frames)
    spread = jnp.sum(centred * centred, axis=0, keepdims=True) * (1.0 / frames)
    scored = (centred * lax.rsqrt(spread + EPSILON)).astype(jnp.bfloat16)
    for g, (first, size) in enumerate(groups):
        gathered[g][col] = scored[first : first + size]
    right_ref[row] = scored

    pl.semaphore_wait(barrier, 4 - jnp.where(is_first, 1, 0) + jnp.where(is_last, 1, 0))
    pl.when(jnp.logical_not(is_last))(lambda: greet(row, above))

    x_pieces = cut(0, frames, X_PIECES)

    def up_copy(g, hop):
        part = gathered[g].at[col_at(1 - hop)]
        return copy(part, part, up_send.at[g, hop - 1], up_recv.at[g, hop - 1], row, above)

    def down_copy(g, hop):
        part = gathered[g].at[col_at(hop - 1)]
        return copy(part, part, down_send.at[g, hop - 1], down_recv.at[g, hop - 1], row, below)

    def far_copy(g, hop):
        part = gathered[g].at[col]
        return copy(part, part, far_send.at[g], up_recv.at[g, hop - 1], row, 0)

    def x_hops(n, way):
        return chips // 2 if n % 2 == way else chips - 1 - chips // 2

    def x_copy(n, way, hop):
        first, size = x_pieces[n]
        origin = 2 * chip_at(1 - hop if way == 0 else hop - 1) + core
        part = right_ref.at[origin, pl.ds(first, size)]
        to_row = 2 * chip_at(1 if way == 0 else -1) + core
        return copy(part, part, x_send.at[n, way, hop - 1], x_recv.at[n, way, hop - 1], to_row, col)

    def d_copy(n, offset):
        first, size = x_pieces[n]
        part = right_ref.at[2 * chip_at(offset) + core, pl.ds(first, size)]
        return copy(part, part, d_send.at[n, offset], d_recv.at[n, offset], partner, col)

    def k_copy(offset):
        return copy(keep_ref, keeps.at[row], k_send.at[offset], k_recv.at[offset], lax.rem(row + offset, rows), col)

    turns = arrivals(cols, chips, behind, ahead)
    held = turns[0][0][0]

    def up_step(hop):
        for g in range(n_g):
            up_copy(g, hop).wait_recv()
            if hop < behind:
                pl.when(jnp.logical_not(is_last))(lambda: up_copy(g, hop + 1).start())
            if hop == 1:

                @pl.when(is_first)
                def _():
                    down_copy(g, 1).start()

        if hop == 1:

            @pl.when(is_first)
            def _():
                for i in range(1, min(held, ahead - 1) + 1):
                    for g in range(n_g):
                        down_copy(g, i + 1).start()

    def down_step(hop):
        for g in range(n_g):
            down_copy(g, hop).wait_recv()
            if hop < ahead:
                if hop <= held:
                    pl.when(jnp.logical_not(is_first))(lambda: down_copy(g, hop + 1).start())
                else:
                    down_copy(g, hop + 1).start()
            if hop == 1:
                pl.when(jnp.logical_not(is_last))(lambda: up_copy(g, 1).start())

    def x_step(hop):
        for n in range(len(x_pieces)):
            for way in range(2):
                if hop <= x_hops(n, way):
                    x_copy(n, way, hop).wait_recv()
                    if hop < x_hops(n, way):
                        x_copy(n, way, hop + 1).start()
                    d_copy(n, chips - hop if way == 0 else hop).start()

    for g in range(n_g):
        pl.when(is_last)(lambda: up_copy(g, 1).start())
        for hop in range(2, behind + 1):
            pl.when(col == cols - hop)(lambda: far_copy(g, hop).start())
    for g in range(n_g):
        pl.when(jnp.logical_not(is_first))(lambda: down_copy(g, 1).start())
    for n in range(len(x_pieces)):
        for way in range(2):
            x_copy(n, way, 1).start()
    for n in range(len(x_pieces)):
        d_copy(n, 0).start()

    same = lax.rem(col, 2) == 0
    to_core = lax.rem(row + col, 2)
    offsets = [0] + sorted(range(1, chips), key=lambda o: (min(o, chips - o), o))
    to_above = offsets[::2]
    loads[1].wait()
    loads[2].wait()

    def picked(k, owner):
        place = jnp.int32(0)
        for i in range(cols):
            place = jnp.where(owner_ref[k * cols + i] == owner, i, place)
        return place

    for turn in range(ahead + 1):
        if turn:
            down_step(turn)
        for hop in range(1, behind + 1):
            at = [c for c in range(cols) if turns[c][0][hop - 1] == turn]
            if at:
                pl.when(functools.reduce(jnp.logical_or, [col == c for c in at]))(functools.partial(up_step, hop))
        for hop in range(1, chips // 2 + 1):
            at = [c for c in range(cols) if turns[c][1][hop - 1] == turn]
            if at:
                pl.when(functools.reduce(jnp.logical_or, [col == c for c in at]))(functools.partial(x_step, hop))
    for n in range(len(x_pieces)):
        for offset in range(chips):
            d_copy(n, offset).wait_recv()

    def a_copy(g, offset):
        return copy(
            outbox[g].at[offset],
            left_ref.at[row, pl.ds(*groups[g])],
            a_send.at[g, offset],
            a_recv.at[g, offset],
            2 * chip_at(offset) + to_core,
            col,
        )

    places = [picked(row, 2 * chip_at(offset) + to_core) for offset in range(chips)]

    def a_start(g):
        for offset in offsets[1:]:
            outbox[g][offset] = gathered[g][places[offset]]
            a_copy(g, offset).start()

        @pl.when(same)
        def _():
            left_ref[row, pl.ds(*groups[g])] = gathered[g][places[0]]

        @pl.when(jnp.logical_not(same))
        def _():
            outbox[g][0] = gathered[g][places[0]]
            a_copy(g, 0).start()

    def e_copy(g, offset, to_col, send):
        part = left_ref.at[2 * chip_at(-offset) + to_core, pl.ds(*groups[g])]
        return copy(part, part, send.at[g, offset], e_recv.at[g, offset], row, to_col)

    def e_start(g):
        for offset in offsets:
            if offset:
                a_copy(g, offset).wait_recv()
            else:
                pl.when(jnp.logical_not(same))(lambda: a_copy(g, 0).wait_recv())
            if offset in to_above:
                pl.when(jnp.logical_not(is_last))(lambda: e_copy(g, offset, above, e_send).start())
                pl.when(col == 1)(lambda: e_copy(g, offset, below, f_send).start())
            else:
                e_copy(g, offset, below, e_send).start()

    for g in range(n_g):
        a_start(g)
        if g == 0:
            keeps[row] = keep_ref[...]
            for offset in range(1, rows):
                k_copy(offset).start()
    for g in range(n_g):
        e_start(g)

    for offset in range(1, rows):
        k_copy(offset).wait_recv()
    spots = jnp.zeros(spots_ref.shape, jnp.int32)
    lane = lax.broadcasted_iota(jnp.int32, spots_ref.shape, 1)
    for k in range(rows):
        place = picked(k, row)
        flags_ref[pl.ds(k, 1), :] = keeps[k, pl.ds(place, 1), :]
        spots = jnp.where(lane == k, place, spots)
    spots_ref[...] = spots
    for g in range(n_g):
        for offset in range(chips):
            e_copy(g, offset, above, e_send).wait_recv()

    for g in range(n_g):
        for hop in range(1, ahead + 1):
            down_copy(g, hop).wait_send()
        up_copy(g, 1).wait_send()
        for hop in range(2, behind + 1):
            pl.when(jnp.logical_not(is_last))(lambda: up_copy(g, hop).wait_send())
            pl.when(col == cols - hop)(lambda: far_copy(g, hop).wait_send())
    for n in range(len(x_pieces)):
        for way in range(2):
            for hop in range(1, x_hops(n, way) + 1):
                x_copy(n, way, hop).wait_send()
        for offset in range(chips):
            d_copy(n, offset).wait_send()
    for offset in range(1, rows):
        k_copy(offset).wait_send()
    for g in range(n_g):
        for offset in range(chips):
            if offset:
                a_copy(g, offset).wait_send()
            else:
                pl.when(jnp.logical_not(same))(lambda: a_copy(g, 0).wait_send())
            if offset in to_above:
                pl.when(jnp.logical_not(is_last))(lambda: e_copy(g, offset, above, e_send).wait_send())
                pl.when(col == 1)(lambda: e_copy(g, offset, below, f_send).wait_send())
            else:
                e_copy(g, offset, below, e_send).wait_send()


def multiply(capacity, limit, left_ref, right_ref, flags_ref, spots_ref, tiles_ref, ids_ref, packed, ids, places, sem):
    rows, frames, tile = left_ref.shape
    cols = flags_ref.shape[1]
    col = lax.axis_index("col")
    total_cols = cols * lax.axis_size("col")
    first_col = col * cols
    for i in range(cols + 1):
        places[i] = 0

    def one_row(k, start):
        count = jnp.int32(0)
        for j in range(cols):
            places[count] = j
            count += flags_ref[k, j]
        base = (k * cols + spots_ref[0, k]) * total_cols + first_col
        rows_of = left_ref[k]
        for s in range(0, limit, 2):
            a, b = places[s], places[s + 1]
            product = lax.dot_general(
                rows_of,
                jnp.concatenate([right_ref[a], right_ref[b]], axis=1),
                (((0,), (0,)), ((), ())),
                preferred_element_type=jnp.float32,
            ) * (1.0 / frames)
            packed[start + s] = product[:, :tile].astype(packed.dtype)
            packed[start + s + 1] = product[:, tile:].astype(packed.dtype)
            ids[start + s] = base + a
            ids[start + s + 1] = base + b
        return start + count

    total = lax.fori_loop(0, rows, one_row, jnp.int32(0))

    def blank(s, carry):
        packed[s] = jnp.zeros_like(packed[s])
        ids[s] = -1
        return carry

    lax.fori_loop(total, capacity, blank, 0)
    out = pltpu.make_async_copy(packed.at[pl.ds(0, capacity)], tiles_ref, sem)
    out.start()
    for s in range(capacity):
        ids_ref[s] = ids[s]
    out.wait()


def shards(series, keep_mask, row_owner):
    frames, tile = series.shape
    row_count, col_count = keep_mask.shape
    rows, cols = lax.axis_size("row"), lax.axis_size("col")
    limit = max(2, 3 * col_count // 8)
    capacity = row_count * limit
    groups = cut(0, frames, GROUPS)
    chips = rows // 2
    vmem, smem, hbm = (pl.BlockSpec(memory_space=m) for m in (pltpu.VMEM, pltpu.SMEM, pltpu.HBM))
    dma = pltpu.SemaphoreType.DMA
    left, right, flags, spots = pl.pallas_call(
        functools.partial(move, rows, cols, groups),
        out_shape=(
            jax.ShapeDtypeStruct((rows, frames, tile), jnp.bfloat16),
            jax.ShapeDtypeStruct((rows, frames, tile), jnp.bfloat16),
            jax.ShapeDtypeStruct((rows, col_count), jnp.int32),
            jax.ShapeDtypeStruct((1, rows), jnp.int32),
        ),
        in_specs=[hbm, hbm, hbm],
        out_specs=(vmem, vmem, vmem, vmem),
        scratch_shapes=[
            *[pltpu.VMEM((cols, size, tile), jnp.bfloat16) for _, size in groups],
            *[pltpu.VMEM((chips, size, tile), jnp.bfloat16) for _, size in groups],
            pltpu.VMEM((frames, tile), series.dtype),
            pltpu.VMEM((row_count, col_count), jnp.int32),
            pltpu.SMEM(row_owner.shape, jnp.int32),
            pltpu.VMEM((rows, row_count, col_count), jnp.int32),
            dma((3,)),
            *[dma((GROUPS, BEHIND))] * 2,
            *[dma((GROUPS, cols - 1 - BEHIND))] * 2,
            dma((GROUPS,)),
            *[dma((X_PIECES, 2, chips // 2))] * 2,
            *[dma((X_PIECES, chips))] * 2,
            *[dma((GROUPS, chips))] * 2,
            *[dma((GROUPS, chips))] * 3,
            *[dma((rows,))] * 2,
        ],
        compiler_params=pltpu.CompilerParams(collective_id=0, has_side_effects=True, vmem_limit_bytes=24 * 2**20),
    )(series, keep_mask, row_owner)
    tiles, ids = pl.pallas_call(
        functools.partial(multiply, capacity, limit),
        out_shape=(
            jax.ShapeDtypeStruct((capacity, tile, tile), jnp.bfloat16),
            jax.ShapeDtypeStruct((capacity,), jnp.int32),
        ),
        in_specs=[vmem, vmem, smem, smem],
        out_specs=(pl.BlockSpec(memory_space=pl.ANY), smem),
        scratch_shapes=[
            pltpu.VMEM((capacity + limit, tile, tile), jnp.bfloat16),
            pltpu.SMEM((capacity + limit,), jnp.int32),
            pltpu.SMEM((col_count + 1,), jnp.int32),
            dma(()),
        ],
        compiler_params=pltpu.CompilerParams(vmem_limit_bytes=24 * 2**20),
    )(left, right, flags, spots)
    return tiles.reshape(1, 1, capacity, tile, tile), ids.reshape(1, 1, capacity)


def solution(mesh):
    in_specs = (P(None, ("subj", "row", "col")), P(("subj", "row"), "col"), P("subj"))
    out_specs = (P(("subj", "row"), "col", None, None, None), P(("subj", "row"), "col", None))
    return jax.shard_map(shards, mesh=mesh, in_specs=in_specs, out_specs=out_specs, check_vma=False)
```

time: 136 us -> 168 us (1.24)
  Pallas kernels: 132 us -> 164 us
    pallas_call x1, Pallas kernels: 122 us -> 154 us  [shards(): pl.pallas_call(functools.partial(move, rows, cols, groups), out_shape=(ja...]
where the time goes in v2:
time: 168 us; the launch traced here: 167 us
  Pallas kernels  164 us (98%)
  local copies, waits for them, and re-layouts  2.37 us (1%)
    pallas_call x1, Pallas kernels, shards(): pl.pallas_call(functools.partial(move, rows, cols, groups), out_shape=(ja...  154 us
    pallas_call x1, Pallas kernels, shards(): pl.pallas_call(functools.partial(multiply, capacity, limit), out_shape=(j...  10.1 us

profile of v2, /device:TPU:65, one launch (start us, length us, event | category | flops | bytes accessed | tf_op | source)
XLA Modules:
  0.0 167.5 jit_solution(5859959812062962313)
XLA Ops:
  0.6 0.0 copy-start
  0.6 1.0 copy-done
  1.6 0.0 copy-start.1
  1.6 0.7 copy-done.1
  2.3 0.0 copy-start.2
  2.3 0.7 copy-done.2
  3.0 154.4 %shard_map.50 = (bf16[16,800,128]{2,1,0:T(8,128)(2,1)S(1)}, bf16[16,800,128]{2,1,0:T(8,128)(2,1)S(1)}, s32[16,16]{1,0:T(8,128)S(1)}, s32[1,16]{1,0:T(1,128)S(1)}) custom-call(f32[800,128]{1,0:T(8,128)S(1)} %copy-done, s32[16,16]{1,0:T(8,128)S(1)} %copy-done.1, s32[256]{0:T(256)S(1)} %copy-done.2), custom_call_target="tpu_custom_call" | custom-call | tf_op jit(solution)/shard_map/pallas_call | solution.py:413
  157.4 10.1 %shard_map.51 = (bf16[96,128,128]{2,1,0:T(8,128)(2,1)}, s32[96]{0:T(128)}) custom-call(bf16[16,800,128]{2,1,0:T(8,128)(2,1)S(1)} %get-tuple-element.8.left_ref, bf16[16,800,128]{2,1,0:T(8,128)(2,1)S(1)} %get-tuple-element.9.right_ref, s32[16,16]{1,0:T(8,128)S(1)} %get-tuple-element.10.flags_ref, s32[1,16]{1,0:T(1,128)S(1)} %get-tuple-element.11.spots_ref), custom_call_target="tpu_custom_call" | custom-call | tf_op jit(solution)/shard_map/pallas_call | solution.py:442
Async XLA Ops:
  0.6 1.0 copy-start
  1.6 0.7 copy-start.1
  2.3 0.7 copy-start.2

commit v3 on v1

--- a/solution.py
+++ b/solution.py
@@ -9,6 +9,7 @@
 
 MESH = pl.DeviceIdType.MESH
 EPSILON = 1e-05
+RUN = 8
 UNIT = 16
 GROUPS = 2
 PIECES = 4
@@ -93,23 +94,23 @@
         g, _, first, size = z_pieces[n]
         origin = col_at(1 - hop if way == 0 else hop - 1)
         part = gathered[g].at[origin, pl.ds(first - groups[g][0][0], size)]
-        return copy(part, part, z_send.at[n, way, hop - 1], z_recv.at[n, way, hop - 1], row, up if way == 0 else down)
+        return copy(part, part, z_send.at[g], z_recv.at[n, way, hop - 1], row, up if way == 0 else down)
 
     def x_copy(n, way, hop):
         first, size = x_pieces[n]
         origin = 2 * chip_at(1 - hop if way == 0 else hop - 1) + core
         part = right_ref.at[origin, pl.ds(first, size)]
         to_row = 2 * chip_at(1 if way == 0 else -1) + core
-        return copy(part, part, x_send.at[n, way, hop - 1], x_recv.at[n, way, hop - 1], to_row, col)
+        return copy(part, part, x_send.at[n], x_recv.at[n, way, hop - 1], to_row, col)
 
     def d_copy(n, offset):
         first, size = x_pieces[n]
         part = right_ref.at[2 * chip_at(offset) + core, pl.ds(first, size)]
-        return copy(part, part, d_send.at[n, offset], d_recv.at[n, offset], partner, col)
+        return copy(part, part, d_send.at[n], d_recv.at[n, offset], partner, col)
 
     def k_copy(offset):
         return copy(
-            keep_ref, keeps.at[row], k_send.at[offset], k_recv.at[offset], lax.rem(row + offset, rows), col
+            keep_ref, keeps.at[row], k_send.at[0], k_recv.at[offset], lax.rem(row + offset, rows), col
         )
 
     def z_start(g):
@@ -146,7 +147,7 @@
         return copy(
             outbox[g].at[offset],
             left_ref.at[row, pl.ds(first, size)],
-            a_send.at[g, offset],
+            a_send.at[g],
             a_recv.at[g, offset],
             2 * chip_at(offset) + to_core,
             col,
@@ -180,7 +181,7 @@
     def e_copy(g, offset):
         first, size = groups[g][0][0], sum(s for _, s in groups[g])
         part = left_ref.at[2 * chip_at(-offset) + to_core, pl.ds(first, size)]
-        return copy(part, part, e_send.at[g, offset], e_recv.at[g, offset], row, up if offset in to_up else down)
+        return copy(part, part, e_send.at[g], e_recv.at[g, offset], row, up if offset in to_up else down)
 
     def e_start(g):
         for offset in offsets:
@@ -233,29 +234,18 @@
         for offset in range(chips):
             e_copy(g, offset).wait_recv()
 
-    for n in range(len(z_pieces)):
-        for way in range(2):
-            for hop in range(1, z_hops(n, way) + 1):
-                z_copy(n, way, hop).wait_send()
-    for n in range(len(x_pieces)):
-        for way in range(2):
-            for hop in range(1, x_hops(n, way) + 1):
-                x_copy(n, way, hop).wait_send()
-        for offset in range(chips):
-            d_copy(n, offset).wait_send()
-    for offset in range(1, rows):
-        k_copy(offset).wait_send()
+    def left(part, sem):
+        copy(part, part, sem, k_recv.at[0], partner, col).wait_send()
+
     for g in range(len(groups)):
-        for offset in range(chips):
-            if offset:
-                a_copy(g, offset).wait_send()
-            else:
-
-                @pl.when(jnp.logical_not(same))
-                def _():
-                    a_copy(g, offset).wait_send()
-
-            e_copy(g, offset).wait_send()
+        span = pl.ds(groups[g][0][0], sum(s for _, s in groups[g]))
+        left(gathered[g].at[pl.ds(0, cols - 1)], z_send.at[g])
+        left(right_ref.at[pl.ds(0, chips - 1), span], x_send.at[g])
+        left(right_ref.at[pl.ds(0, chips), span], d_send.at[g])
+        pl.when(same)(lambda: left(outbox[g].at[pl.ds(0, chips - 1)], a_send.at[g]))
+        pl.when(jnp.logical_not(same))(lambda: left(outbox[g], a_send.at[g]))
+        left(left_ref.at[pl.ds(0, chips), span], e_send.at[g])
+    left(keeps.at[pl.ds(0, rows - 1)], k_send.at[0])
 
 
 def multiply(capacity, limit, left_ref, right_ref, flags_ref, owner_ref, tiles_ref, ids_ref, packed, ids, places, sem):
@@ -267,7 +257,15 @@
     for i in range(cols + 1):
         places[i] = 0
 
-    def one_row(k, start):
+    def put(i):
+        run = pl.ds(i * RUN, RUN)
+        return pltpu.make_async_copy(packed.at[run], tiles_ref.at[run], sem)
+
+    def put_runs(first, end):
+        lax.fori_loop(first, end, lambda i, carry: put(i).start(), None)
+
+    start, sent = jnp.int32(0), jnp.int32(0)
+    for k in range(rows):
         count = jnp.int32(0)
         for j in range(cols):
             places[count] = j
@@ -276,34 +274,32 @@
         for i in range(cols):
             place = jnp.where(owner_ref[k * cols + i] == row, i, place)
         base = (k * cols + place) * total_cols + first_col
-        rows_of = left_ref[k]
-        for s in range(0, limit, 2):
-            a, b = places[s], places[s + 1]
-            product = lax.dot_general(
-                rows_of,
-                jnp.concatenate([right_ref[a], right_ref[b]], axis=1),
-                (((0,), (0,)), ((), ())),
-                preferred_element_type=jnp.float32,
-            ) * (1.0 / frames)
-            packed[start + s] = product[:, :tile].astype(packed.dtype)
-            packed[start + s + 1] = product[:, tile:].astype(packed.dtype)
-            ids[start + s] = base + a
-            ids[start + s + 1] = base + b
-        return start + count
-
-    total = lax.fori_loop(0, rows, one_row, jnp.int32(0))
+        kept = [places[s] for s in range(limit)]
+        product = lax.dot_general(
+            left_ref[k],
+            jnp.concatenate([right_ref[j] for j in kept], axis=1),
+            (((0,), (0,)), ((), ())),
+            preferred_element_type=jnp.float32,
+        ) * (1.0 / frames)
+        for s, j in enumerate(kept):
+            packed[start + s] = product[:, s * tile : (s + 1) * tile].astype(packed.dtype)
+            ids[start + s] = base + j
+        start += count
+        if k % 4 == 3 and k + 1 < rows:
+            ready = lax.div(start, RUN)
+            put_runs(sent, ready)
+            sent = ready
 
     def blank(s, carry):
         packed[s] = jnp.zeros_like(packed[s])
         ids[s] = -1
         return carry
 
-    lax.fori_loop(total, capacity, blank, 0)
-    out = pltpu.make_async_copy(packed.at[pl.ds(0, capacity)], tiles_ref, sem)
-    out.start()
+    lax.fori_loop(start, capacity, blank, 0)
+    put_runs(sent, capacity // RUN)
     for s in range(capacity):
         ids_ref[s] = ids[s]
-    out.wait()
+    pltpu.make_async_copy(packed.at[pl.ds(0, capacity)], tiles_ref, sem).wait()
 
 
 def shards(series, keep_mask, row_owner):
@@ -331,12 +327,13 @@
             *[pltpu.VMEM((cols, size, tile), jnp.bfloat16) for size in sizes],
             *[pltpu.VMEM((chips, size, tile), jnp.bfloat16) for size in sizes],
             pltpu.VMEM((rows, row_count, col_count), jnp.int32),
-            *[dma((n_z, 2, cols // 2))] * 2,
-            *[dma((n_g, 2, chips // 2))] * 2,
-            *[dma((n_g, chips))] * 2,
-            *[dma((n_g, chips))] * 2,
-            *[dma((n_g, chips))] * 2,
-            *[dma((rows,))] * 2,
+            dma((n_g,)),
+            dma((n_z, 2, cols // 2)),
+            dma((n_g,)),
+            dma((n_g, 2, chips // 2)),
+            *[dma((n_g,)), dma((n_g, chips))] * 3,
+            dma((1,)),
+            dma((rows,)),
         ],
         compiler_params=pltpu.CompilerParams(collective_id=0, has_side_effects=True, vmem_limit_bytes=24 * 2**20),
     )(series, keep_mask, row_owner)

time: 136 us -> 131 us (0.963)
  Pallas kernels: 132 us -> 127 us
    pallas_call x1, Pallas kernels: 9.81 us -> 7.24 us  [shards(): pl.pallas_call(functools.partial(multiply, capacity, limit), out_shape=(j...]
    pallas_call x1, Pallas kernels: 122 us -> 120 us  [shards(): pl.pallas_call(functools.partial(move, rows, cols, groups), out_shape=(ja...]
where the time goes in v3:
time: 131 us; the launch traced here: 130 us
  Pallas kernels  127 us (97%)
  local copies, waits for them, and re-layouts  2.37 us (2%)
    pallas_call x1, Pallas kernels, shards(): pl.pallas_call(functools.partial(move, rows, cols, groups), out_shape=(ja...  120 us
    pallas_call x1, Pallas kernels, shards(): pl.pallas_call(functools.partial(multiply, capacity, limit), out_shape=(j...  7.24 us

profile of v3, /device:TPU:65, one launch (start us, length us, event | category | flops | bytes accessed | tf_op | source)
XLA Modules:
  0.0 129.8 jit_solution(6072737392357277117)
XLA Ops:
  0.6 0.0 copy-start
  0.6 1.0 copy-done
  1.6 0.0 copy-start.1
  1.6 0.7 copy-done.1
  2.3 0.0 copy-start.2
  2.3 0.7 copy-done.2
  3.0 119.6 %shard_map.50 = (bf16[16,800,128]{2,1,0:T(8,128)(2,1)S(1)}, bf16[16,800,128]{2,1,0:T(8,128)(2,1)S(1)}, s32[16,16]{1,0:T(8,128)S(1)}) custom-call(f32[800,128]{1,0:T(8,128)S(1)} %copy-done, s32[16,16]{1,0:T(8,128)S(1)} %copy-done.1, s32[256]{0:T(256)S(1)} %copy-done.2), custom_call_target="tpu_custom_call" | custom-call | tf_op jit(solution)/shard_map/pallas_call | solution.py:317
  122.6 7.2 %shard_map.51 = (bf16[96,128,128]{2,1,0:T(8,128)(2,1)}, s32[96]{0:T(128)}) custom-call(bf16[16,800,128]{2,1,0:T(8,128)(2,1)S(1)} %get-tuple-element.7.left_ref, bf16[16,800,128]{2,1,0:T(8,128)(2,1)S(1)} %get-tuple-element.8.right_ref, s32[16,16]{1,0:T(8,128)S(1)} %get-tuple-element.9.flags_ref, s32[256]{0:T(256)S(1)} %copy-done.2), custom_call_target="tpu_custom_call" | custom-call | tf_op jit(solution)/shard_map/pallas_call | solution.py:340
Async XLA Ops:
  0.6 1.0 copy-start
  1.6 0.7 copy-start.1
  2.3 0.7 copy-start.2

commit v4 on v3

--- a/solution.py
+++ b/solution.py
@@ -11,8 +11,11 @@
 EPSILON = 1e-05
 RUN = 8
 UNIT = 16
-GROUPS = 2
-PIECES = 4
+GROUPS = 4
+LAG = 2
+EARLY = 4
+X_PIECES = 2
+PIECES = 2
 
 
 def cut(first, size, parts):
@@ -61,10 +64,8 @@
         )
 
     barrier = pltpu.get_barrier_semaphore()
-    for offset in range(1, rows):
-        pl.semaphore_signal(
-            barrier, inc=1, device_id={"row": lax.rem(row + offset, rows), "col": col}, device_id_type=MESH
-        )
+    for to_row in (2 * chip_at(1) + core, 2 * chip_at(-1) + core, partner):
+        pl.semaphore_signal(barrier, inc=1, device_id={"row": to_row, "col": col}, device_id_type=MESH)
     for to_col in (up, down):
         pl.semaphore_signal(barrier, inc=1, device_id={"row": row, "col": to_col}, device_id_type=MESH)
 
@@ -79,10 +80,10 @@
     right_ref[row] = scored
     keeps[row] = keep_ref[...]
 
-    pl.semaphore_wait(barrier, rows + 1)
+    pl.semaphore_wait(barrier, 5)
 
     z_pieces = [(g, i, *piece) for g, pieces in enumerate(groups) for i, piece in enumerate(pieces)]
-    x_pieces = [(pieces[0][0], sum(s for _, s in pieces)) for pieces in groups]
+    x_pieces = cut(0, series_ref.shape[0], X_PIECES)
 
     def z_hops(n, way):
         return cols // 2 if n % 2 == way else cols - 1 - cols // 2
@@ -196,29 +197,36 @@
             e_copy(g, offset).start()
 
     last = cols // 2
+    x_turns = [last * (i + 1) * 3 // (2 * chips) + 1 for i in range(chips // 2)]
     z_start(0)
     for n in range(len(x_pieces)):
         for way in range(2):
             x_copy(n, way, 1).start()
-    for offset in range(1, rows):
-        k_copy(offset).start()
     for n in range(len(x_pieces)):
         d_copy(n, 0).start()
-    for g in range(len(groups)):
-        for hop in range(1, last):
-            z_step(g, hop)
-            if g == 0 and hop % 2 == 0:
-                x_step(hop // 2)
-        if g + 1 < len(groups):
-            z_start(g + 1)
-        z_step(g, last)
-        if g == 0:
-            for hop in range(last // 2, chips // 2 + 1):
-                x_step(hop)
-        a_start(g)
-        if g:
-            e_start(g - 1)
-    e_start(len(groups) - 1)
+    for turn in range(1, last + LAG * (len(groups) - 1) + 1):
+        for g in range(len(groups)):
+            hop = turn - LAG * g
+            if hop == 0:
+                z_start(g)
+            if 1 <= hop <= last:
+                z_step(g, hop)
+        if turn in x_turns:
+            x_step(x_turns.index(turn) + 1)
+        for g in range(len(groups)):
+            if turn - LAG * g == last:
+                if g == 0:
+                    for n in range(len(x_pieces)):
+                        for offset in range(chips):
+                            d_copy(n, offset).wait_recv()
+                a_start(g)
+                if g == 0:
+                    for offset in range(1, rows):
+                        k_copy(offset).start()
+                if g >= EARLY:
+                    e_start(g - EARLY)
+    for g in range(max(0, len(groups) - EARLY), len(groups)):
+        e_start(g)
 
     for offset in range(1, rows):
         k_copy(offset).wait_recv()
@@ -227,9 +235,6 @@
         for i in range(cols):
             place = jnp.where(owner_ref[k * cols + i] == row, i, place)
         flags_ref[pl.ds(k, 1), :] = keeps[k, pl.ds(place, 1), :]
-    for n in range(len(x_pieces)):
-        for offset in range(chips):
-            d_copy(n, offset).wait_recv()
     for g in range(len(groups)):
         for offset in range(chips):
             e_copy(g, offset).wait_recv()
@@ -240,11 +245,12 @@
     for g in range(len(groups)):
         span = pl.ds(groups[g][0][0], sum(s for _, s in groups[g]))
         left(gathered[g].at[pl.ds(0, cols - 1)], z_send.at[g])
-        left(right_ref.at[pl.ds(0, chips - 1), span], x_send.at[g])
-        left(right_ref.at[pl.ds(0, chips), span], d_send.at[g])
         pl.when(same)(lambda: left(outbox[g].at[pl.ds(0, chips - 1)], a_send.at[g]))
         pl.when(jnp.logical_not(same))(lambda: left(outbox[g], a_send.at[g]))
         left(left_ref.at[pl.ds(0, chips), span], e_send.at[g])
+    for n, piece in enumerate(x_pieces):
+        left(right_ref.at[pl.ds(0, chips - 1), pl.ds(*piece)], x_send.at[n])
+        left(right_ref.at[pl.ds(0, chips), pl.ds(*piece)], d_send.at[n])
     left(keeps.at[pl.ds(0, rows - 1)], k_send.at[0])
 
 
@@ -329,9 +335,11 @@
             pltpu.VMEM((rows, row_count, col_count), jnp.int32),
             dma((n_g,)),
             dma((n_z, 2, cols // 2)),
-            dma((n_g,)),
-            dma((n_g, 2, chips // 2)),
-            *[dma((n_g,)), dma((n_g, chips))] * 3,
+            dma((X_PIECES,)),
+            dma((X_PIECES, 2, chips // 2)),
+            dma((X_PIECES,)),
+            dma((X_PIECES, chips)),
+            *[dma((n_g,)), dma((n_g, chips))] * 2,
             dma((1,)),
             dma((rows,)),
         ],

time: 131 us -> 133 us (1.015)
  Pallas kernels: 127 us -> 129 us
    pallas_call x1, Pallas kernels: 120 us -> 122 us  [shards(): pl.pallas_call(functools.partial(move, rows, cols, groups), out_shape=(ja...]
where the time goes in v4:
time: 133 us; the launch traced here: 132 us
  Pallas kernels  129 us (97%)
  local copies, waits for them, and re-layouts  2.37 us (2%)
    pallas_call x1, Pallas kernels, shards(): pl.pallas_call(functools.partial(move, rows, cols, groups), out_shape=(ja...  122 us
    pallas_call x1, Pallas kernels, shards(): pl.pallas_call(functools.partial(multiply, capacity, limit), out_shape=(j...  7.01 us

profile of v4, /device:TPU:65, one launch (start us, length us, event | category | flops | bytes accessed | tf_op | source)
XLA Modules:
  0.0 132.3 jit_solution(9776074413699919676)
XLA Ops:
  0.6 0.0 copy-start
  0.6 1.0 copy-done
  1.6 0.0 copy-start.1
  1.6 0.7 copy-done.1
  2.3 0.0 copy-start.2
  2.3 0.7 copy-done.2
  3.0 122.3 %shard_map.50 = (bf16[16,800,128]{2,1,0:T(8,128)(2,1)S(1)}, bf16[16,800,128]{2,1,0:T(8,128)(2,1)S(1)}, s32[16,16]{1,0:T(8,128)S(1)}) custom-call(f32[800,128]{1,0:T(8,128)S(1)} %copy-done, s32[16,16]{1,0:T(8,128)S(1)} %copy-done.1, s32[256]{0:T(256)S(1)} %copy-done.2), custom_call_target="tpu_custom_call" | custom-call | tf_op jit(solution)/shard_map/pallas_call | solution.py:323
  125.3 7.0 %shard_map.51 = (bf16[96,128,128]{2,1,0:T(8,128)(2,1)}, s32[96]{0:T(128)}) custom-call(bf16[16,800,128]{2,1,0:T(8,128)(2,1)S(1)} %get-tuple-element.7.left_ref, bf16[16,800,128]{2,1,0:T(8,128)(2,1)S(1)} %get-tuple-element.8.right_ref, s32[16,16]{1,0:T(8,128)S(1)} %get-tuple-element.9.flags_ref, s32[256]{0:T(256)S(1)} %copy-done.2), custom_call_target="tpu_custom_call" | custom-call | tf_op jit(solution)/shard_map/pallas_call | solution.py:348
Async XLA Ops:
  0.6 1.0 copy-start
  1.6 0.7 copy-start.1
  2.3 0.7 copy-start.2

commit v5 on v4

--- a/solution.py
+++ b/solution.py
@@ -13,7 +13,6 @@
 UNIT = 16
 GROUPS = 4
 LAG = 2
-EARLY = 4
 X_PIECES = 2
 PIECES = 2
 
@@ -64,8 +63,10 @@
         )
 
     barrier = pltpu.get_barrier_semaphore()
-    for to_row in (2 * chip_at(1) + core, 2 * chip_at(-1) + core, partner):
-        pl.semaphore_signal(barrier, inc=1, device_id={"row": to_row, "col": col}, device_id_type=MESH)
+    for offset in range(1, rows):
+        pl.semaphore_signal(
+            barrier, inc=1, device_id={"row": lax.rem(row + offset, rows), "col": col}, device_id_type=MESH
+        )
     for to_col in (up, down):
         pl.semaphore_signal(barrier, inc=1, device_id={"row": row, "col": to_col}, device_id_type=MESH)
 
@@ -80,7 +81,7 @@
     right_ref[row] = scored
     keeps[row] = keep_ref[...]
 
-    pl.semaphore_wait(barrier, 5)
+    pl.semaphore_wait(barrier, rows + 1)
 
     z_pieces = [(g, i, *piece) for g, pieces in enumerate(groups) for i, piece in enumerate(pieces)]
     x_pieces = cut(0, series_ref.shape[0], X_PIECES)
@@ -197,11 +198,12 @@
             e_copy(g, offset).start()
 
     last = cols // 2
-    x_turns = [last * (i + 1) * 3 // (2 * chips) + 1 for i in range(chips // 2)]
     z_start(0)
     for n in range(len(x_pieces)):
         for way in range(2):
             x_copy(n, way, 1).start()
+    for offset in range(1, rows):
+        k_copy(offset).start()
     for n in range(len(x_pieces)):
         d_copy(n, 0).start()
     for turn in range(1, last + LAG * (len(groups) - 1) + 1):
@@ -211,21 +213,12 @@
                 z_start(g)
             if 1 <= hop <= last:
                 z_step(g, hop)
-        if turn in x_turns:
-            x_step(x_turns.index(turn) + 1)
+        if turn <= last and turn % 2 == 0:
+            x_step(turn // 2)
         for g in range(len(groups)):
             if turn - LAG * g == last:
-                if g == 0:
-                    for n in range(len(x_pieces)):
-                        for offset in range(chips):
-                            d_copy(n, offset).wait_recv()
                 a_start(g)
-                if g == 0:
-                    for offset in range(1, rows):
-                        k_copy(offset).start()
-                if g >= EARLY:
-                    e_start(g - EARLY)
-    for g in range(max(0, len(groups) - EARLY), len(groups)):
+    for g in range(len(groups)):
         e_start(g)
 
     for offset in range(1, rows):
@@ -235,6 +228,9 @@
         for i in range(cols):
             place = jnp.where(owner_ref[k * cols + i] == row, i, place)
         flags_ref[pl.ds(k, 1), :] = keeps[k, pl.ds(place, 1), :]
+    for n in range(len(x_pieces)):
+        for offset in range(chips):
+            d_copy(n, offset).wait_recv()
     for g in range(len(groups)):
         for offset in range(chips):
             e_copy(g, offset).wait_recv()

time: 133 us -> 129 us (0.970)
  Pallas kernels: 129 us -> 126 us
    pallas_call x1, Pallas kernels: 122 us -> 118 us  [shards(): pl.pallas_call(functools.partial(move, rows, cols, groups), out_shape=(ja...]
where the time goes in v5:
time: 129 us
  Pallas kernels  126 us (98%)
  local copies, waits for them, and re-layouts  2.37 us (2%)
    pallas_call x1, Pallas kernels, shards(): pl.pallas_call(functools.partial(move, rows, cols, groups), out_shape=(ja...  118 us
    pallas_call x1, Pallas kernels, shards(): pl.pallas_call(functools.partial(multiply, capacity, limit), out_shape=(j...  7.8 us

profile of v5, /device:TPU:65, one launch (start us, length us, event | category | flops | bytes accessed | tf_op | source)
XLA Modules:
  0.0 129.0 jit_solution(892942034333889254)
XLA Ops:
  0.6 0.0 copy-start
  0.6 1.0 copy-done
  1.6 0.0 copy-start.1
  1.6 0.7 copy-done.1
  2.3 0.0 copy-start.2
  2.3 0.7 copy-done.2
  3.0 118.2 %shard_map.50 = (bf16[16,800,128]{2,1,0:T(8,128)(2,1)S(1)}, bf16[16,800,128]{2,1,0:T(8,128)(2,1)S(1)}, s32[16,16]{1,0:T(8,128)S(1)}) custom-call(f32[800,128]{1,0:T(8,128)S(1)} %copy-done, s32[16,16]{1,0:T(8,128)S(1)} %copy-done.1, s32[256]{0:T(256)S(1)} %copy-done.2), custom_call_target="tpu_custom_call" | custom-call | tf_op jit(solution)/shard_map/pallas_call | solution.py:319
  121.2 7.8 %shard_map.51 = (bf16[96,128,128]{2,1,0:T(8,128)(2,1)}, s32[96]{0:T(128)}) custom-call(bf16[16,800,128]{2,1,0:T(8,128)(2,1)S(1)} %get-tuple-element.7.left_ref, bf16[16,800,128]{2,1,0:T(8,128)(2,1)S(1)} %get-tuple-element.8.right_ref, s32[16,16]{1,0:T(8,128)S(1)} %get-tuple-element.9.flags_ref, s32[256]{0:T(256)S(1)} %copy-done.2), custom_call_target="tpu_custom_call" | custom-call | tf_op jit(solution)/shard_map/pallas_call | solution.py:344
Async XLA Ops:
  0.6 1.0 copy-start
  1.6 0.7 copy-start.1
  2.3 0.7 copy-start.2
